TPU v7x, 512 devices: a whole 4x4x16 slice. The times are simulated.
512 devices in a mesh: tau: 8 (over z_lo), row: 8 (over y, core), col: 8 (over x, z_hi).
Axes of the slice: x: 4, y: 4, z: 16 (z_hi: 2, z_lo: 8; z = z_hi * 8 + z_lo), core: 2. Of those that a mesh axis runs over, the one named last changes fastest.
Arguments:
- occupied: bfloat16 [8, 1024, 8192], P('tau', 'row', 'col'), may hold values from -6 to 6
- virtual_green: bfloat16 [8, 8192, 2048], P('tau', 'row', 'col'), may hold values from -0.0625 to 0.0625
- occ_mask: int32 [8, 64], P('row', 'col'), may hold values 0 or 1
- virt_mask: int32 [64, 16], P('row', 'col'), may hold values 0 or 1
- chi_mask: int32 [8, 16], P('row', 'col'), may hold values 0 or 1
- cosine_weights: float32 [8, 8], replicated, may hold values from -3 to 3
Outputs:
- chi_freq: float32 [8, 1024, 2048], P(None, ('row', 'tau'), 'col')
All inputs are finite; a program needn't handle non-finite values. No bound on the sum of `occ_mask` or of `virt_mask` or of `chi_mask` on one device may be relied on, other than what follows from the above.
Results may differ from a plain program's by a relative error of at most 0.0029.
Values may be sent and summed in bfloat16 or wider, within the bound.
A program may use at most 64 MiB of HBM per device.

v0:
```python
import jax
import jax.numpy as jnp
from jax import lax
from jax.sharding import PartitionSpec as P


def copy_for_each(value, axis):
    count = lax.axis_size(axis)
    return lax.all_to_all(
        jnp.broadcast_to(value[None], (count, *value.shape)), axis, 0, 0, tiled=True
    )


def joined_along(blocks, dim):
    shape = list(blocks.shape[1:])
    shape[dim] *= blocks.shape[0]
    return jnp.moveaxis(blocks, 0, dim).reshape(shape)


def collect(value, axis, dim):
    blocks = copy_for_each(value, axis)
    return joined_along(blocks, dim)


def expand_mask(values, flags):
    block_rows = values.shape[0] // flags.shape[0]
    block_cols = values.shape[1] // flags.shape[1]
    shaped = values.reshape(flags.shape[0], block_rows, flags.shape[1], block_cols)
    masked = shaped * flags.astype(values.dtype)[:, None, :, None]
    return masked.reshape(values.shape)


def shards(occupied, virtual_green, occ_mask, virt_mask, chi_mask, cosine_weights):
    occ_tile = expand_mask(occupied[0], occ_mask)
    virt_tile = expand_mask(virtual_green[0], virt_mask)
    virt_column = lax.all_gather(virt_tile, "row", axis=0, tiled=True)
    accumulated = jnp.dot(
        collect(occ_tile, "col", 1), virt_column, preferred_element_type=jnp.float32
    )
    chi_local = expand_mask(accumulated, chi_mask).astype(jnp.bfloat16)
    regrouped = lax.all_to_all(chi_local[None], "tau", split_axis=1, concat_axis=0, tiled=True)
    return jnp.einsum(
        "kt,tij->kij",
        cosine_weights,
        regrouped.astype(jnp.float32),
        precision=lax.Precision.HIGHEST,
    )


def solution(mesh):
    placed = (
        P("tau", "row", "col"),
        P("tau", "row", "col"),
        P("row", "col"),
        P("row", "col"),
        P("row", "col"),
        P(),
    )
    return jax.shard_map(
        shards,
        mesh=mesh,
        in_specs=placed,
        out_specs=P(None, ("row", "tau"), "col"),
        check_vma=False,
    )
```

profile of v0, /device:TPU:8, one launch (start us, length us, event | category | flops | bytes accessed | tf_op | source)
XLA Modules:
  0.0 165.8 jit_solution(2362016631813210816)
XLA Ops:
  6.5 0.0 copy-start
  6.5 0.0 copy-start.2
  6.5 0.0 copy-start.1
  6.5 0.0 all-gather.2.cloned.1.call-start
  6.5 0.7 convert_element_type.24
  7.3 0.1 copy.16
  7.4 0.3 mul.44
  7.7 1.9 %bitcast_multiply_fusion = bf16[1024,256]{1,0:T(8,128)(2,1)} fusion(bf16[128,8,2,128]{3,2,1,0:T(2,128)(2,1)S(1)} %bitcast.31, bf16[1,1024,256]{2,1,0:T(8,128)(2,1)} %param.7), kind=kLoop, calls=%fused_computation.3 | loop fusion | flops 262144 | bytes 1572864 | tf_op jit(solution)/shard_map/mul | solution.py:29
  9.6 0.0 all-gather.2.cloned.1.call-update
  9.7 0.0 copy-done.2
  9.7 0.1 broadcast_bitcast_fusion
  9.8 0.0 copy-done.1
  9.8 1.6 broadcast_in_dim.5
  11.4 0.0 copy-start.3
  11.4 17.7 %all-to-all-start = ((bf16[8,128,1024]{2,1,0:T(8,128)(2,1)}), bf16[8,128,1024]{2,1,0:T(8,128)(2,1)S(1)}, u32[]{:S(2)}, u32[]{:S(2)}) async-start(bf16[8,128,1024]{2,1,0:T(8,128)(2,1)} %broadcast_in_dim.5), calls=%async_computation | async-start | bytes 4194304 | tf_op jit(solution)/shard_map/all_to_all | solution.py:9
  29.1 0.0 copy-done.3
  29.1 23.8 %all-gather.2.cloned.1.call-done = bf16[8192,256]{1,0:T(8,128)(2,1)} async-done(((bf16[1024,256]{1,0:T(8,128)(2,1)}), bf16[8192,256]{1,0:T(8,128)(2,1)}) %all-gather.2.cloned.1.call-update) | async-done | bytes 4194320 | tf_op jit(solution)/shard_map/all_gather | solution.py:36
  52.9 6.4 %copy.17 = bf16[256,8192]{1,0:T(8,128)(2,1)} copy(bf16[256,8192]{0,1:T(8,128)(2,1)} %bitcast.30) | data formatting | bytes 8388608 | tf_op jit(solution)/shard_map/dot_general | solution.py:37
  59.3 19.7 %all-to-all-done = bf16[8,128,1024]{2,1,0:T(8,128)(2,1)S(1)} async-done(((bf16[8,128,1024]{2,1,0:T(8,128)(2,1)}), bf16[8,128,1024]{2,1,0:T(8,128)(2,1)S(1)}, u32[]{:S(2)}, u32[]{:S(2)}) %all-to-all-start) | async-done | bytes 2097184 | tf_op jit(solution)/shard_map/all_to_all | solution.py:9
  79.0 2.5 %copy.15 = bf16[128,8,1024]{2,1,0:T(8,128)(2,1)} copy(bf16[128,8,1024]{2,0,1:T(8,128)(2,1)S(1)} %bitcast.29) | data formatting | bytes 4194304 | tf_op jit(solution)/shard_map/transpose | solution.py:17
  81.5 2.9 %reshape.38 = bf16[128,8192,1]{1,0,2:T(8,128)(2,1)S(1)} reshape(bf16[128,8,1024]{2,1,0:T(8,128)(2,1)} %copy.15) | data formatting | bytes 4194304 | tf_op jit(solution)/shard_map/reshape | solution.py:17
  84.3 3.4 %fusion = bf16[128,2,128]{0,2,1:T(8,128)(2,1)S(1)} fusion(bf16[128,8192,1]{1,0,2:T(8,128)(2,1)S(1)} %reshape.38, bf16[2,128,8192]{2,1,0:T(8,128)(2,1)} %bitcast.28, f32[2]{0:T(128)S(1)} %convert_bitcast_fusion), kind=kOutput, calls=%fused_computation.2 | convolution fusion | flops 536936448 | bytes 6357000 | tf_op jit(solution)/shard_map/dot_general | solution.py:37
  87.8 0.1 copy.18
  87.9 0.5 broadcast.9
  88.4 1.0 reduce
  89.5 68.5 %all_to_all.17 = bf16[8,2,2048]{2,1,0:T(2,128)(2,1)S(1)} all-to-all(bf16[8,2,2048]{2,1,0:T(2,128)(2,1)S(1)} %reshape.41), channel_id=1, replica_groups=mesh['tau'=8,'row'=8,'col'=8] {'tau'}, dimensions={0} | all-to-all | bytes 131072 | tf_op jit(solution)/shard_map/all_to_all | solution.py:41
  158.0 0.1 reshape.42
  158.1 0.0 copy-done
  158.1 0.2 convolution_bitcast_fusion
  158.3 0.7 copy.20
  (5 shorter events, 0.1 us)
Async XLA Ops:
  6.5 151.6 %copy-start = (f32[8,8]{1,0:T(8,128)S(1)}, f32[8,8]{1,0:T(8,128)}, u32[]{:S(2)}) copy-start(f32[8,8]{1,0:T(8,128)} %param.11) | copy-start | bytes 772
  6.5 3.1 %copy-start.2 = (s32[1,8]{1,0:T(1,128)S(1)}, s32[1,8]{1,0:T(1,128)}, u32[]{:S(2)}) copy-start(s32[1,8]{1,0:T(1,128)} %param.8) | copy-start | bytes 100
  6.5 3.2 %copy-start.1 = (bf16[1,128,1024]{2,1,0:T(8,128)(2,1)S(1)}, bf16[1,128,1024]{2,1,0:T(8,128)(2,1)}, u32[]{:S(2)}) copy-start(bf16[1,128,1024]{2,1,0:T(8,128)(2,1)} %param.6) | copy-start | bytes 786436
  6.5 46.4 %all-gather.2.cloned.1.call-start = ((), (), s32[]{:S(2)}) async-start(), calls=%async_computation.2 | async-start | bytes 4718592 | tf_op jit(solution)/shard_map/all_gather | solution.py:36
  11.4 17.7 %copy-start.3 = (s32[1,2]{1,0:T(1,128)S(1)}, s32[1,2]{1,0:T(1,128)}, u32[]{:S(2)}) copy-start(s32[1,2]{1,0:T(1,128)} %param.10) | copy-start | bytes 28
  11.4 67.6 %all-to-all-start = ((bf16[8,128,1024]{2,1,0:T(8,128)(2,1)}), bf16[8,128,1024]{2,1,0:T(8,128)(2,1)S(1)}, u32[]{:S(2)}, u32[]{:S(2)}) async-start(bf16[8,128,1024]{2,1,0:T(8,128)(2,1)} %broadcast_in_dim.5), calls=%async_computation | async-start | bytes 4194304 | tf_op jit(solution)/shard_map/all_to_all | solution.py:9
Sparse Core Ops, SparseCore 0:
  9.8 43.0 all-gather.1
where the time goes:
time: 166 us
  blocking collectives  68.5 us (41%)
  waiting for transfers between devices  43.5 us (26%)
  starting transfers between devices  17.7 us (11%)
  local copies, waits for them, and re-layouts  15.3 us (9%)
  between operations  13.5 us (8%)
  other arithmetic  3.7 us (2%)
  matrix products  3.64 us (2%)
    all_to_all x1, blocking collectives, shards(): lax.all_to_all(chi_local[None], 'tau', split_axis=1, concat_axis=0, tiled...  68.5 us
    all_gather x1, waiting for transfers between devices, shards(): virt_column = lax.all_gather(virt_tile, 'row', axis=0, tiled=True)  23.8 us
    all_to_all x1, waiting for transfers between devices, copy_for_each(): lax.all_to_all(jnp.broadcast_to(value[None], (count, *value.shape)), axis...  19.7 us
    all_to_all x1, starting transfers between devices, copy_for_each(): lax.all_to_all(jnp.broadcast_to(value[None], (count, *value.shape)), axis...  17.7 us
    dot_general x1, local copies, waits for them, and re-layouts, shards(): jnp.dot(collect(occ_tile, 'col', 1), virt_column, preferred_element_type=...  6.39 us
    dot_general x1, matrix products, shards(): jnp.dot(collect(occ_tile, 'col', 1), virt_column, preferred_element_type=...  3.45 us
  transfers between devices with their start and end apart: 2, of which 2 were waited for; matrix products, arithmetic and copies ran while one was open for 5% of the time, Pallas kernels for 0%

commit v1 on v0

--- a/solution.py
+++ b/solution.py
@@ -2,6 +2,19 @@
 import jax.numpy as jnp
 from jax import lax
 from jax.sharding import PartitionSpec as P
+
+
+def collect_2(value, axis, dim):
+    ways = lax.axis_size(axis)
+    up = [(d, (d + 1) % ways) for d in range(ways)]
+    down = [(d, (d - 1) % ways) for d in range(ways)]
+    earlier, later = ([value], [value])
+    for _ in range(ways // 2):
+        earlier.append(lax.ppermute(earlier[-1], axis, up))
+    for _ in range((ways - 1) // 2):
+        later.append(lax.ppermute(later[-1], axis, down))
+    line = jnp.concatenate([*earlier[::-1], *later[1:]], axis=dim)
+    return jnp.roll(line, (lax.axis_index(axis) - ways // 2) * value.shape[dim], axis=dim)
 
 
 def copy_for_each(value, axis):
@@ -33,7 +46,7 @@
 def shards(occupied, virtual_green, occ_mask, virt_mask, chi_mask, cosine_weights):
     occ_tile = expand_mask(occupied[0], occ_mask)
     virt_tile = expand_mask(virtual_green[0], virt_mask)
-    virt_column = lax.all_gather(virt_tile, "row", axis=0, tiled=True)
+    virt_column = collect_2(virt_tile, "row", 0)
     accumulated = jnp.dot(
         collect(occ_tile, "col", 1), virt_column, preferred_element_type=jnp.float32
     )

time: 166 us -> 152 us (0.916)
  waiting for transfers between devices: 43.5 us -> 28.8 us
  between operations: 13.5 us -> 0.2 us
  local copies, waits for them, and re-layouts: 15.3 us -> 28.3 us
  blocking collectives: 68.5 us -> 62.6 us
  starting transfers between devices: 17.7 us -> 22.8 us
    ppermute x0 -> x7, waiting for transfers between devices: none -> 28.8 us  [the longest x4 28.5 us: collect_2(): earlier.append(lax.ppermute(earlier[-1], axis, up))]
    all_gather x1 -> x0, waiting for transfers between devices: 23.8 us -> none  [shards(): virt_column = lax.all_gather(virt_tile, 'row', axis=0, tiled=True)]
    all_to_all x1, waiting for transfers between devices: 19.7 us -> 0.01 us  [copy_for_each(): lax.all_to_all(jnp.broadcast_to(value[None], (count, *value.shape)), axis...]
    unnamed x12 -> x27, local copies, waits for them, and re-layouts: 0.63 us -> 11.3 us
    all_to_all x1, blocking collectives: 68.5 us -> 62.6 us  [shards(): lax.all_to_all(chi_local[None], 'tau', split_axis=1, concat_axis=0, tiled...]
    ppermute x0 -> x7, starting transfers between devices: none -> 5.23 us  [the longest x3 5.21 us: collect_2(): later.append(lax.ppermute(later[-1], axis, down))]
    dot_general x1 -> x2, local copies, waits for them, and re-layouts: 6.39 us -> 8.67 us  [shards(): jnp.dot(collect(occ_tile, 'col', 1), virt_column, preferred_element_type=...]
  transfers between devices with their start and end apart: 2 -> 8, of which waited for: 2 -> 5; matrix products, arithmetic and copies ran while one was open for 5% -> 14% of each run, Pallas kernels for 0% -> 0%
where the time goes in v1:
time: 152 us; the launch traced here: 151 us
  blocking collectives  62.6 us (41%)
  waiting for transfers between devices  28.8 us (19%)
  local copies, waits for them, and re-layouts  28.3 us (19%)
  starting transfers between devices  22.8 us (15%)
  other arithmetic  4.49 us (3%)
  matrix products  3.63 us (2%)
    all_to_all x1, blocking collectives, shards(): lax.all_to_all(chi_local[None], 'tau', split_axis=1, concat_axis=0, tiled...  62.6 us
    ppermute x4, waiting for transfers between devices, collect_2(): earlier.append(lax.ppermute(earlier[-1], axis, up))  28.5 us
    all_to_all x1, starting transfers between devices, copy_for_each(): lax.all_to_all(jnp.broadcast_to(value[None], (count, *value.shape)), axis...  17.6 us
    unnamed x27, local copies, waits for them, and re-layouts  11.3 us
    dot_general x2, local copies, waits for them, and re-layouts, shards(): jnp.dot(collect(occ_tile, 'col', 1), virt_column, preferred_element_type=...  8.67 us
    ppermute x3, starting transfers between devices, collect_2(): later.append(lax.ppermute(later[-1], axis, down))  5.21 us
    dot_general x1, matrix products, shards(): jnp.dot(collect(occ_tile, 'col', 1), virt_column, preferred_element_type=...  3.44 us
  transfers between devices with their start and end apart: 8, of which 5 were waited for; matrix products, arithmetic and copies ran while one was open for 14% of the time, Pallas kernels for 0%

profile of v1, /device:TPU:8, one launch (start us, length us, event | category | flops | bytes accessed | tf_op | source)
XLA Modules:
  0.0 150.8 jit_solution(9291422406510855570)
XLA Ops:
  0.0 0.0 copy-start
  0.0 0.0 copy-start.3
  0.0 0.7 convert_bitcast_fusion.1
  0.7 0.1 broadcast_bitcast_fusion
  0.8 1.0 multiply_bitcast_fusion
  1.7 1.6 %broadcast_in_dim.5 = bf16[8,128,1024]{2,1,0:T(8,128)(2,1)} broadcast(bf16[128,1024]{1,0:T(8,128)(2,1)S(1)} %multiply_bitcast_fusion), dimensions={1,2} | broadcast | bytes 2359296 | tf_op jit(solution)/shard_map/broadcast_in_dim | solution.py:23
  3.4 17.6 %all-to-all-start = ((bf16[8,128,1024]{2,1,0:T(8,128)(2,1)}), bf16[8,128,1024]{2,1,0:T(8,128)(2,1)S(1)}, u32[]{:S(2)}, u32[]{:S(2)}) async-start(bf16[8,128,1024]{2,1,0:T(8,128)(2,1)} %broadcast_in_dim.5), calls=%async_computation | async-start | bytes 4194304 | tf_op jit(solution)/shard_map/all_to_all | solution.py:22
  20.9 0.7 convert_element_type.24
  21.6 0.1 copy.16
  21.7 0.3 mul.47
  22.0 1.1 bitcast_multiply_fusion
  23.2 0.0 collective-permute-start
  23.2 8.6 %collective-permute-done = bf16[1024,256]{1,0:T(8,128)(2,1)S(1)} collective-permute-done((bf16[1024,256]{1,0:T(8,128)(2,1)S(1)}, bf16[1024,256]{1,0:T(8,128)(2,1)S(1)}, u32[]{:S(2)}, u32[]{:S(2)}) %collective-permute-start) | collective-permute-done | bytes 524320 | tf_op jit(solution)/shard_map/ppermute | solution.py:13
  31.8 0.0 collective-permute-start.1
  31.8 1.7 %collective-permute-start.4 = (bf16[1024,256]{1,0:T(8,128)(2,1)S(1)}, bf16[1024,256]{1,0:T(8,128)(2,1)}, u32[]{:S(2)}, u32[]{:S(2)}) collective-permute-start(bf16[1024,256]{1,0:T(8,128)(2,1)S(1)} %bitcast_multiply_fusion), channel_id=1, source_target_pairs={{0,56},{8,0},{16,8},{24,16},{32,24},{40,32},{48,40},{56,48},{1,57}... | collective-permute-start | bytes 1572872 | tf_op jit(solution)/shard_map/ppermute | solution.py:15
  33.5 6.9 %collective-permute-done.1 = bf16[1024,256]{1,0:T(8,128)(2,1)S(1)} collective-permute-done((bf16[1024,256]{1,0:T(8,128)(2,1)S(1)}, bf16[1024,256]{1,0:T(8,128)(2,1)S(1)}, u32[]{:S(2)}, u32[]{:S(2)}) %collective-permute-start.1) | collective-permute-done | bytes 524320 | tf_op jit(solution)/shard_map/ppermute | solution.py:13
  40.4 0.0 copy-start.1
  40.4 0.0 collective-permute-start.2
  40.4 0.0 collective-permute-done.4
  40.4 0.8 copy-done.1
  41.2 1.3 collective-permute-start.5
  42.5 6.7 %collective-permute-done.2 = bf16[1024,256]{1,0:T(8,128)(2,1)} collective-permute-done((bf16[1024,256]{1,0:T(8,128)(2,1)S(1)}, bf16[1024,256]{1,0:T(8,128)(2,1)}, u32[]{:S(2)}, u32[]{:S(2)}) %collective-permute-start.2) | collective-permute-done | bytes 524320 | tf_op jit(solution)/shard_map/ppermute | solution.py:13
  49.1 0.0 collective-permute-start.3
  49.1 0.0 copy-done.3
  49.1 0.0 copy-start.2
  49.1 0.3 collective-permute-done.5
  49.5 2.2 %collective-permute-start.6 = (bf16[1024,256]{1,0:T(8,128)(2,1)}, bf16[1024,256]{1,0:T(8,128)(2,1)S(1)}, u32[]{:S(2)}, u32[]{:S(2)}) collective-permute-start(bf16[1024,256]{1,0:T(8,128)(2,1)} %collective-permute-done.5), channel_id=1, source_target_pairs={{0,56},{8,0},{16,8},{24,16},{32,24},{40,32},{48,40},{56,48},{1,57}... | collective-permute-start | bytes 1572872 | tf_op jit(solution)/shard_map/ppermute | solution.py:15
  51.7 6.4 %collective-permute-done.3 = bf16[1024,256]{1,0:T(8,128)(2,1)} collective-permute-done((bf16[1024,256]{1,0:T(8,128)(2,1)}, bf16[1024,256]{1,0:T(8,128)(2,1)}, u32[]{:S(2)}, u32[]{:S(2)}) %collective-permute-start.3) | collective-permute-done | bytes 524320 | tf_op jit(solution)/shard_map/ppermute | solution.py:13
  58.0 1.1 constant_dynamic-update-slice_fusion.15
  59.1 1.1 constant_dynamic-update-slice_fusion.14
  60.2 1.1 constant_dynamic-update-slice_fusion.13
  61.4 1.1 constant_dynamic-update-slice_fusion.10
  62.5 1.1 constant_dynamic-update-slice_fusion.9
  63.5 0.0 collective-permute-done.6
  63.6 1.1 constant_dynamic-update-slice_fusion.7
  64.7 1.1 constant_dynamic-update-slice_fusion.6
  65.7 0.0 copy-done.2
  65.9 1.1 constant_dynamic-update-slice_fusion.2
  67.0 1.1 constant_dynamic-update-slice_fusion.1
  68.1 2.2 %dynamic-slice_bitcast_fusion = bf16[256,8192]{0,1:T(8,128)(2,1)} fusion(bf16[16384,256]{1,0:T(8,128)(2,1)S(1)} %constant_dynamic-update-slice_fusion, s32[]{:T(128)S(6)} %select_n.14), kind=kLoop, calls=%fused_computation | loop fusion | bytes 8388612 | tf_op jit(solution)/shard_map/dot_general | solution.py:50
  70.3 6.4 %copy.17 = bf16[256,8192]{1,0:T(8,128)(2,1)} copy(bf16[256,8192]{0,1:T(8,128)(2,1)} %dynamic-slice_bitcast_fusion) | data formatting | bytes 8388608 | tf_op jit(solution)/shard_map/dot_general | solution.py:50
  76.8 0.0 all-to-all-done
  76.8 2.5 %copy.15 = bf16[128,8,1024]{2,1,0:T(8,128)(2,1)} copy(bf16[128,8,1024]{2,0,1:T(8,128)(2,1)S(1)} %bitcast.30) | data formatting | bytes 4194304 | tf_op jit(solution)/shard_map/transpose | solution.py:30
  79.3 2.9 %reshape.38 = bf16[128,8192,1]{1,0,2:T(8,128)(2,1)S(1)} reshape(bf16[128,8,1024]{2,1,0:T(8,128)(2,1)} %copy.15) | data formatting | bytes 4194304 | tf_op jit(solution)/shard_map/reshape | solution.py:30
  82.1 3.4 %fusion = bf16[128,2,128]{0,2,1:T(8,128)(2,1)S(1)} fusion(bf16[128,8192,1]{1,0,2:T(8,128)(2,1)S(1)} %reshape.38, bf16[2,128,8192]{2,1,0:T(8,128)(2,1)} %bitcast.29, f32[2]{0:T(128)S(1)} %convert_bitcast_fusion), kind=kOutput, calls=%fused_computation.3 | convolution fusion | flops 536936448 | bytes 6357000 | tf_op jit(solution)/shard_map/dot_general | solution.py:50
  85.6 0.1 copy.18
  85.7 0.5 broadcast.10
  86.2 1.0 reduce
  87.3 62.6 %all_to_all.17 = bf16[8,2,2048]{2,1,0:T(2,128)(2,1)S(1)} all-to-all(bf16[8,2,2048]{2,1,0:T(2,128)(2,1)S(1)} %reshape.41), channel_id=1, replica_groups=mesh['tau'=8,'row'=8,'col'=8] {'tau'}, dimensions={0} | all-to-all | bytes 131072 | tf_op jit(solution)/shard_map/all_to_all | solution.py:54
  149.8 0.1 reshape.42
  149.9 0.0 copy-done
  149.9 0.2 convolution_bitcast_fusion
  150.1 0.7 copy.20
  (10 shorter events, 0.3 us)
Async XLA Ops:
  0.0 149.9 %copy-start = (f32[8,8]{1,0:T(8,128)S(1)}, f32[8,8]{1,0:T(8,128)}, u32[]{:S(2)}) copy-start(f32[8,8]{1,0:T(8,128)} %param.11) | copy-start | bytes 772
  0.0 49.1 %copy-start.3 = (s32[1,2]{1,0:T(1,128)S(1)}, s32[1,2]{1,0:T(1,128)}, u32[]{:S(2)}) copy-start(s32[1,2]{1,0:T(1,128)} %param.10) | copy-start | bytes 28
  3.4 73.4 %all-to-all-start = ((bf16[8,128,1024]{2,1,0:T(8,128)(2,1)}), bf16[8,128,1024]{2,1,0:T(8,128)(2,1)S(1)}, u32[]{:S(2)}, u32[]{:S(2)}) async-start(bf16[8,128,1024]{2,1,0:T(8,128)(2,1)} %broadcast_in_dim.5), calls=%async_computation | async-start | bytes 4194304 | tf_op jit(solution)/shard_map/all_to_all | solution.py:22
  23.2 8.6 %collective-permute-start = (bf16[1024,256]{1,0:T(8,128)(2,1)S(1)}, bf16[1024,256]{1,0:T(8,128)(2,1)S(1)}, u32[]{:S(2)}, u32[]{:S(2)}) collective-permute-start(bf16[1024,256]{1,0:T(8,128)(2,1)S(1)} %bitcast_multiply_fusion), channel_id=1, source_target_pairs={{0,8},{8,16},{16,24},{24,32},{32,40},{40,48},{48,56},{56,0},{1,9},... | collective-permute-start | bytes 1572872 | tf_op jit(solution)/shard_map/ppermute | solution.py:13
  31.8 8.6 %collective-permute-start.1 = (bf16[1024,256]{1,0:T(8,128)(2,1)S(1)}, bf16[1024,256]{1,0:T(8,128)(2,1)S(1)}, u32[]{:S(2)}, u32[]{:S(2)}) collective-permute-start(bf16[1024,256]{1,0:T(8,128)(2,1)S(1)} %collective-permute-done), channel_id=1, source_target_pairs={{0,8},{8,16},{16,24},{24,32},{32,40},{40,48},{48,56},{56,0},{1,9},... | collective-permute-start | bytes 1572872 | tf_op jit(solution)/shard_map/ppermute | solution.py:13
  31.8 8.6 %collective-permute-start.4 = (bf16[1024,256]{1,0:T(8,128)(2,1)S(1)}, bf16[1024,256]{1,0:T(8,128)(2,1)}, u32[]{:S(2)}, u32[]{:S(2)}) collective-permute-start(bf16[1024,256]{1,0:T(8,128)(2,1)S(1)} %bitcast_multiply_fusion), channel_id=1, source_target_pairs={{0,56},{8,0},{16,8},{24,16},{32,24},{40,32},{48,40},{56,48},{1,57}... | collective-permute-start | bytes 1572872 | tf_op jit(solution)/shard_map/ppermute | solution.py:15
  40.4 0.8 copy-start.1
  40.4 8.7 %collective-permute-start.2 = (bf16[1024,256]{1,0:T(8,128)(2,1)S(1)}, bf16[1024,256]{1,0:T(8,128)(2,1)}, u32[]{:S(2)}, u32[]{:S(2)}) collective-permute-start(bf16[1024,256]{1,0:T(8,128)(2,1)S(1)} %collective-permute-done.1), channel_id=1, source_target_pairs={{0,8},{8,16},{16,24},{24,32},{32,40},{40,48},{48,56},{56,0},{1,9},... | collective-permute-start | bytes 1572872 | tf_op jit(solution)/shard_map/ppermute | solution.py:13
  41.2 8.3 %collective-permute-start.5 = (bf16[1024,256]{1,0:T(8,128)(2,1)}, bf16[1024,256]{1,0:T(8,128)(2,1)}, u32[]{:S(2)}, u32[]{:S(2)}) collective-permute-start(bf16[1024,256]{1,0:T(8,128)(2,1)} %collective-permute-done.4), channel_id=1, source_target_pairs={{0,56},{8,0},{16,8},{24,16},{32,24},{40,32},{48,40},{56,48},{1,57}... | collective-permute-start | bytes 1572872 | tf_op jit(solution)/shard_map/ppermute | solution.py:15
  49.1 8.9 %collective-permute-start.3 = (bf16[1024,256]{1,0:T(8,128)(2,1)}, bf16[1024,256]{1,0:T(8,128)(2,1)}, u32[]{:S(2)}, u32[]{:S(2)}) collective-permute-start(bf16[1024,256]{1,0:T(8,128)(2,1)} %collective-permute-done.2), channel_id=1, source_target_pairs={{0,8},{8,16},{16,24},{24,32},{32,40},{40,48},{48,56},{56,0},{1,9},... | collective-permute-start | bytes 1572872 | tf_op jit(solution)/shard_map/ppermute | solution.py:13
  49.1 16.6 %copy-start.2 = (bf16[1024,256]{1,0:T(8,128)(2,1)S(1)}, bf16[1024,256]{1,0:T(8,128)(2,1)}, u32[]{:S(2)}) copy-start(bf16[1024,256]{1,0:T(8,128)(2,1)} %copy-done.1) | copy-start | bytes 1572868
  49.5 14.1 %collective-permute-start.6 = (bf16[1024,256]{1,0:T(8,128)(2,1)}, bf16[1024,256]{1,0:T(8,128)(2,1)S(1)}, u32[]{:S(2)}, u32[]{:S(2)}) collective-permute-start(bf16[1024,256]{1,0:T(8,128)(2,1)} %collective-permute-done.5), channel_id=1, source_target_pairs={{0,56},{8,0},{16,8},{24,16},{32,24},{40,32},{48,40},{56,48},{1,57}... | collective-permute-start | bytes 1572872 | tf_op jit(solution)/shard_map/ppermute | solution.py:15
